TPU v7x, 32 devices: a whole 2x2x4 slice. The times are simulated.
32 devices in a mesh: copy: 2 (over core), shard: 4 (over y, x), cols: 4 (over z).
Axes of the slice: x: 2, y: 2, z: 4, core: 2. Of those that a mesh axis runs over, the one named last changes fastest.
Arguments:
- train_gate: float32 [5120, 9728], P(('copy', 'shard'), 'cols'), parts along dimension 0, may hold values from -0.15625 to 0.15625
- drift_gate: float32 [5120, 9728], P(('copy', 'shard'), 'cols'), parts along dimension 0, may hold values from -6 to 6
- spread_gate: float32 [5120, 9728], P(('copy', 'shard'), 'cols'), parts along dimension 0, may hold values from 0.1 to 10
- train_up: float32 [5120, 9728], P(('copy', 'shard'), 'cols'), parts along dimension 0, may hold values from -0.15625 to 0.15625
- drift_up: float32 [5120, 9728], P(('copy', 'shard'), 'cols'), parts along dimension 0, may hold values from -6 to 6
- spread_up: float32 [5120, 9728], P(('copy', 'shard'), 'cols'), parts along dimension 0, may hold values from 0.1 to 10
- norm_train: float32 [5120], P(('copy', 'shard', 'cols')), parts along dimension 0, may hold values from 0.25 to 1.75
- norm_step: float32 [5120], P(('copy', 'shard', 'cols')), parts along dimension 0, may hold values from -0.3 to 0.3
Outputs:
- final_gate: bfloat16 [5120, 9728], P('copy', 'cols'), parts along dimension 0
- final_up: bfloat16 [5120, 9728], P('copy', 'cols'), parts along dimension 0
- column_gate: float32 [19456], P(('copy', 'cols')), parts along dimension 0
- column_up: float32 [19456], P(('copy', 'cols')), parts along dimension 0
- serve_norm: bfloat16 [5120], P('copy'), parts along dimension 0
- result_gate: float32 [5120, 9728], P(('copy', 'shard'), 'cols'), parts along dimension 0
- result_up: float32 [5120, 9728], P(('copy', 'shard'), 'cols'), parts along dimension 0
There are 2 independent parts, one for each index of `copy`. A program takes and returns all parts, laid end to end along the dimension named above; each array names one. Nothing has to cross between parts.
All inputs are finite; a program needn't handle non-finite values.
Results may differ from a plain program's by a relative error of at most 0.0004.
Values may be sent and summed in bfloat16 or wider, within the bound.
A program may use at most 192 MiB of HBM per device.

v0:
```python
import jax
import jax.numpy as jnp
from jax import lax
from jax.sharding import PartitionSpec as P

learn_rate = 0.015
decay_rate = 0.1
tiny_value = 1e-08


def local(
    train_gate, drift_gate, spread_gate, train_up, drift_up, spread_up, norm_train, norm_step
):
    result_gate = train_gate - learn_rate * (
        drift_gate / (jnp.sqrt(spread_gate) + tiny_value) + decay_rate * train_gate
    )
    result_up = train_up - learn_rate * (
        drift_up / (jnp.sqrt(spread_up) + tiny_value) + decay_rate * train_up
    )
    total_gate, total_up = lax.psum(
        (jnp.sum(result_gate * result_gate, axis=0), jnp.sum(result_up * result_up, axis=0)),
        "shard",
    )
    column_gate = jnp.sqrt(total_gate)
    column_up = jnp.sqrt(total_up)
    narrow_gate, narrow_up = (
        (result_gate / column_gate).astype(jnp.bfloat16),
        (result_up / column_up).astype(jnp.bfloat16),
    )
    final_gate, final_up = (
        lax.all_gather(narrow_gate, "shard", axis=0, tiled=True),
        lax.all_gather(narrow_up, "shard", axis=0, tiled=True),
    )
    serve_norm = lax.all_gather(
        (norm_train + norm_step).astype(jnp.bfloat16), ("shard", "cols"), axis=0, tiled=True
    )
    return (final_gate, final_up, column_gate, column_up, serve_norm, result_gate, result_up)


def solution(mesh):
    return jax.shard_map(
        local,
        mesh=mesh,
        in_specs=(
            P(("copy", "shard"), "cols"),
            P(("copy", "shard"), "cols"),
            P(("copy", "shard"), "cols"),
            P(("copy", "shard"), "cols"),
            P(("copy", "shard"), "cols"),
            P(("copy", "shard"), "cols"),
            P(("copy", "shard", "cols")),
            P(("copy", "shard", "cols")),
        ),
        out_specs=(
            P("copy", "cols"),
            P("copy", "cols"),
            P(("copy", "cols")),
            P(("copy", "cols")),
            P("copy"),
            P(("copy", "shard"), "cols"),
            P(("copy", "shard"), "cols"),
        ),
        check_vma=False,
    )
```

profile of v0, /device:TPU:0, one launch (start us, length us, event | category | flops | bytes accessed | tf_op | source)
XLA Modules:
  0.0 319.7 jit_solution(6063659269506991792)
XLA Ops:
  7.2 0.0 all-gather.5.cloned.1.call-start
  7.2 19.9 %multiply_reduce_fusion = (f32[2432]{0:T(1024)S(1)}, f32[640,2432]{1,0:T(8,128)}, f32[2432]{0:T(1024)S(1)}, f32[640,2432]{1,0:T(8,128)}) fusion(f32[640,2432]{1,0:T(8,128)} %param.11, f32[640,2432]{1,0:T(8,128)} %param.12, f32[640,2432]{1,0:T(8,128)} %param.13, f32[640,2432]{1,0:T(8,128)} %param.8, f32[640,2432]{1,0:T(8,128)} %param.9, f32[640,2432]{1,0:T(8,128)} %param.10), kind=kLoop, calls=%fused_computation.1 | loop fusion | flops 24898816 | bytes 49826816 | tf_op jit(solution)/shard_map/reduce_sum | solution.py:21
  27.1 17.7 %all-reduce.1 = (f32[2432]{0:T(1024)S(1)}, f32[2432]{0:T(1024)S(1)}) all-reduce(f32[2432]{0:T(1024)S(1)} %get-tuple-element.13, f32[2432]{0:T(1024)S(1)} %get-tuple-element.9), channel_id=1, replica_groups=mesh['copy'=2,'shard'=4,'cols'=4] {'shard'}, use_global_device_ids=true, to_apply=%region_1.0 | all-reduce | flops 4864 | bytes 38912 | tf_op jit(solution)/shard_map/psum | solution.py:20
  44.8 0.0 copy-start.1
  44.8 4.8 %divide_convert_fusion = bf16[640,2432]{1,0:T(8,128)(2,1)} fusion(f32[640,2432]{1,0:T(8,128)} %get-tuple-element.28, f32[2432]{0:T(1024)S(1)} %sqrt.15), kind=kLoop, calls=%fused_computation | loop fusion | flops 3112960 | bytes 9348608 | tf_op jit(solution)/shard_map/convert_element_type | solution.py:28
  49.7 0.0 all-gather.5.cloned.1.call-update
  49.7 0.0 copy-done.1
  49.7 0.0 all-gather.3.cloned.1.call-start
  49.8 0.0 copy-start.2
  49.8 0.0 copy-start.5
  49.8 0.0 copy-start.3
  49.8 0.0 copy-start.4
  49.8 4.8 %divide_convert_fusion.1 = bf16[640,2432]{1,0:T(8,128)(2,1)} fusion(f32[640,2432]{1,0:T(8,128)} %get-tuple-element.27, f32[2432]{0:T(1024)S(1)} %sqrt.13), kind=kLoop, calls=%fused_computation.3 | loop fusion | flops 3112960 | bytes 9348608 | tf_op jit(solution)/shard_map/convert_element_type | solution.py:27
  54.6 0.0 all-gather.3.cloned.1.call-update
  54.7 0.0 copy-done.2
  54.7 0.0 copy-done.5
  54.7 0.6 dynamic-slice
  56.0 0.2 dynamic-update-slice
  56.2 42.3 %all-reduce = bf16[2560]{0:T(1024)(128)(2,1)} all-reduce(bf16[2560]{0:T(1024)(128)(2,1)S(1)} %dynamic-update-slice), channel_id=1, replica_groups=mesh['copy'=2,'shard'=4,'cols'=4] {'shard','cols'}, use_global_device_ids=true, to_apply=%add | all-reduce | flops 2560 | bytes 10240
  98.5 73.1 %all-gather.5.cloned.1.call-done = bf16[2560,2432]{1,0:T(8,128)(2,1)} async-done(((bf16[640,2432]{1,0:T(8,128)(2,1)}), bf16[2560,2432]{1,0:T(8,128)(2,1)}) %all-gather.5.cloned.1.call-update) | async-done | bytes 12451856 | tf_op jit(solution)/shard_map/all_gather | solution.py:32
  171.6 123.7 %all-gather.3.cloned.1.call-done = bf16[2560,2432]{1,0:T(8,128)(2,1)} async-done(((bf16[640,2432]{1,0:T(8,128)(2,1)}), bf16[2560,2432]{1,0:T(8,128)(2,1)}) %all-gather.3.cloned.1.call-update) | async-done | bytes 12451856 | tf_op jit(solution)/shard_map/all_gather | solution.py:31
  295.4 11.0 %copy.18 = bf16[2560,2432]{1,0:T(8,128)(2,1)} copy(bf16[2560,2432]{1,0:T(8,128)(2,1)} %all-gather.3.cloned.1.call-done) | data formatting | bytes 24903680
  306.4 1.8 copy-done
  308.2 4.7 %copy.19 = bf16[2560,2432]{1,0:T(8,128)(2,1)} copy(bf16[2560,2432]{1,0:T(8,128)(2,1)S(1)} %copy-done) | data formatting | bytes 24903680
  (7 shorter events, 0.0 us)
Async XLA Ops:
  7.2 164.5 %all-gather.5.cloned.1.call-start = ((), (), s32[]{:S(2)}) async-start(), calls=%async_computation.1 | async-start | bytes 15564800 | tf_op jit(solution)/shard_map/all_gather | solution.py:32
  44.8 4.9 %copy-start.1 = (f32[2432]{0:T(1024)}, f32[2432]{0:T(1024)S(1)}, u32[]{:S(2)}) copy-start(f32[2432]{0:T(1024)S(1)} %sqrt.15) | copy-start | bytes 29188
  49.7 245.7 %all-gather.3.cloned.1.call-start = ((), (), s32[]{:S(2)}) async-start(), calls=%async_computation | async-start | bytes 15564800 | tf_op jit(solution)/shard_map/all_gather | solution.py:31
  49.8 4.9 %copy-start.2 = (f32[2432]{0:T(1024)}, f32[2432]{0:T(1024)S(1)}, u32[]{:S(2)}) copy-start(f32[2432]{0:T(1024)S(1)} %sqrt.13) | copy-start | bytes 29188
  49.8 4.9 %copy-start.5 = (u32[32]{0:T(128)S(1)}, u32[32]{0:T(128)}, u32[]{:S(2)}) copy-start(u32[32]{0:T(128)} %constant.10) | copy-start | bytes 388
  49.8 6.2 %copy-start.3 = (f32[160]{0:T(256)S(1)}, f32[160]{0:T(256)}, u32[]{:S(2)}) copy-start(f32[160]{0:T(256)} %param.14) | copy-start | bytes 1924
  49.8 6.2 %copy-start.4 = (f32[160]{0:T(256)S(1)}, f32[160]{0:T(256)}, u32[]{:S(2)}) copy-start(f32[160]{0:T(256)} %param.15) | copy-start | bytes 1924
  295.4 12.8 %copy-start = (bf16[2560,2432]{1,0:T(8,128)(2,1)S(1)}, bf16[2560,2432]{1,0:T(8,128)(2,1)}, u32[]{:S(2)}) copy-start(bf16[2560,2432]{1,0:T(8,128)(2,1)} %all-gather.5.cloned.1.call-done) | copy-start | bytes 37355524
Sparse Core Ops, SparseCore 0:
  49.8 121.7 all-gather.4
  174.0 121.2 all-gather.2
where the time goes:
time: 320 us
  waiting for transfers between devices  197 us (62%)
  blocking collectives  60 us (19%)
  other arithmetic  29.6 us (9%)
  local copies, waits for them, and re-layouts  18.4 us (6%)
  between operations  14.8 us (5%)
    all_gather x1, waiting for transfers between devices, local(): lax.all_gather(narrow_gate, 'shard', axis=0, tiled=True)  124 us
    all_gather x1, waiting for transfers between devices, local(): lax.all_gather(narrow_up, 'shard', axis=0, tiled=True)  73.1 us
    unnamed x1, blocking collectives  42.3 us
    reduce_sum x1, other arithmetic, local(): jnp.sum(result_up * result_up, axis=0)  19.9 us
    unnamed x17, local copies, waits for them, and re-layouts  18.4 us
    psum x1, blocking collectives, local(): lax.psum((jnp.sum(result_gate * result_gate, axis=0), jnp.sum(result_up *...  17.7 us
  transfers between devices with their start and end apart: 2, of which 2 were waited for; matrix products, arithmetic and copies ran while one was open for 2% of the time, Pallas kernels for 0%

commit v1 on v0

v1 whole, which is shorter than its diff:
```python
import functools

import jax
import jax.numpy as jnp
from jax import lax
from jax.experimental import pallas as pl
from jax.experimental.pallas import tpu as pltpu
from jax.sharding import PartitionSpec as P

learn_rate = 0.015
decay_rate = 0.1
tiny_value = 1e-08
LANES = 128
BLOCK = 64
LAG = 3
MESH = pl.DeviceIdType.MESH


def stepped(train, drift, spread):
    return train - learn_rate * (
        drift / (jnp.sqrt(spread) + tiny_value) + decay_rate * train
    )


def plain(
    train_gate, drift_gate, spread_gate, train_up, drift_up, spread_up, norm_train, norm_step
):
    result_gate = stepped(train_gate, drift_gate, spread_gate)
    result_up = stepped(train_up, drift_up, spread_up)
    total_gate, total_up = lax.psum(
        (jnp.sum(result_gate * result_gate, axis=0), jnp.sum(result_up * result_up, axis=0)),
        "shard",
    )
    column_gate = jnp.sqrt(total_gate)
    column_up = jnp.sqrt(total_up)
    narrow_gate = (result_gate / column_gate).astype(jnp.bfloat16)
    narrow_up = (result_up / column_up).astype(jnp.bfloat16)
    final_gate = lax.all_gather(narrow_gate, "shard", axis=0, tiled=True)
    final_up = lax.all_gather(narrow_up, "shard", axis=0, tiled=True)
    serve_norm = lax.all_gather(
        (norm_train + norm_step).astype(jnp.bfloat16), ("shard", "cols"), axis=0, tiled=True
    )
    return (final_gate, final_up, column_gate, column_up, serve_norm, result_gate, result_up)


def gather_kernel(
    chunks, ncols,
    tg, dg, sg, tu, du, su, norm_a, norm_b,
    T, R, col, N,
    inbuf, res, own, part, gain,
    in_sem, res_sem, loc_sem, psend, precv, osend, orecv, fsend, frecv, nsend, nrecv,
):
    ins = (tg, dg, sg, tu, du, su)
    rows = tg.shape[0]
    me = lax.axis_index("shard")
    mc = lax.axis_index("cols")
    mx = lax.rem(me, 2)
    my = me // 2
    nx = my * 2 + (1 - mx)
    ny = (1 - my) * 2 + mx
    nd = (1 - my) * 2 + (1 - mx)
    peers = (nx, ny, nd)

    def fetch(c, slot):
        return [
            pltpu.make_async_copy(
                ins[k].at[:, pl.ds(pl.multiple_of(c * LANES, LANES), LANES)],
                inbuf.at[slot, k],
                in_sem.at[slot, k],
            )
            for k in range(6)
        ]

    for f in fetch(0, 0):
        f.start()

    everyone = [(i, j) for i in range(4) for j in range(ncols) if i or j]

    def other(i, j):
        return {"shard": lax.rem(me + i, 4), "cols": lax.rem(mc + j, ncols)}

    barrier = pltpu.get_barrier_semaphore()
    for i, j in everyone:
        pl.semaphore_signal(barrier, inc=1, device_id=other(i, j), device_id_type=MESH)
    pl.semaphore_wait(barrier, len(everyone))

    def remote(src, dst, send, recv, shard):
        return pltpu.make_async_remote_copy(
            src_ref=src, dst_ref=dst, send_sem=send, recv_sem=recv,
            device_id={"shard": shard}, device_id_type=MESH,
        )

    def share(c, k):
        return remote(part.at[c, me], part.at[c, me], psend.at[c, k], precv.at[c, k], peers[k])

    def share_in(c, k):
        return remote(part.at[c, peers[k]], part.at[c, peers[k]], psend.at[c, k], precv.at[c, k], peers[k])

    def give(c, k):
        return remote(own.at[c], T.at[c, me], osend.at[c, k], orecv.at[c, k], peers[k])

    def give_in(c, k):
        return remote(own.at[c], T.at[c, peers[k]], osend.at[c, k], orecv.at[c, k], peers[k])

    def pass_on(c, k):
        return remote(
            T.at[c, peers[1 - k], 1 - k], T.at[c, peers[1 - k], 1 - k],
            fsend.at[c, k], frecv.at[c, k], peers[k],
        )

    def pass_in(c, k):
        return remote(
            T.at[c, nd, 1 - k], T.at[c, nd, 1 - k],
            fsend.at[c, k], frecv.at[c, k], peers[k],
        )

    def save(c):
        return pltpu.make_async_copy(res.at[c], R.at[c], res_sem.at[c])

    def keep(c):
        return pltpu.make_async_copy(own.at[c], T.at[c, me], loc_sem.at[c])

    def stage_a(c):
        slot = lax.rem(c, 2)
        for f in fetch(c, slot):
            f.wait()

        @pl.when(c + 1 < chunks)
        def _():
            for f in fetch(c + 1, 1 - slot):
                f.start()

        for g in range(2):
            def body(i, acc):
                at = pl.ds(pl.multiple_of(i * BLOCK, BLOCK), BLOCK)
                value = stepped(
                    inbuf[slot, 3 * g, at, :], inbuf[slot, 3 * g + 1, at, :], inbuf[slot, 3 * g + 2, at, :]
                )
                res[c, g, at, :] = value
                return acc + jnp.sum((value * value).reshape(BLOCK // 8, 8, LANES), axis=0)

            acc = lax.fori_loop(0, rows // BLOCK, body, jnp.zeros((8, LANES), jnp.float32))
            part[c, me, pl.ds(g, 1), :] = jnp.sum(acc, axis=0, keepdims=True)
        for k in range(3):
            share(c, k).start()
        save(c).start()

    def stage_b(c):
        for k in range(3):
            share_in(c, k).wait_recv()
        scale = jnp.sqrt(part[c, 0] + part[c, 1] + part[c, 2] + part[c, 3])
        col[c] = scale
        for g in range(2):
            divisor = scale[g : g + 1, :]

            def body(i, _):
                at = pl.ds(pl.multiple_of(i * BLOCK, BLOCK), BLOCK)
                own[c, g, at, :] = (res[c, g, at, :] / divisor).astype(jnp.bfloat16)
                return 0

            lax.fori_loop(0, rows // BLOCK, body, 0)
        for k in range(2):
            give(c, k).start()
        keep(c).start()

    def stage_c(c):
        for k in range(2):
            give_in(c, k).wait_recv()
            pass_on(c, 1 - k).start()

    stage_a(0)

    mine = me * ncols + mc
    gain[mine] = (norm_a[...] + norm_b[...]).astype(jnp.bfloat16)

    def gain_copy(n, i, j):
        to = other(i, j)
        return pltpu.make_async_remote_copy(
            src_ref=gain.at[mine], dst_ref=gain.at[mine],
            send_sem=nsend.at[n], recv_sem=nrecv.at[n], device_id=to, device_id_type=MESH,
        )

    def gain_in(n, i, j):
        source = lax.rem(me + 4 - i, 4) * ncols + lax.rem(mc + ncols - j, ncols)
        return pltpu.make_async_remote_copy(
            src_ref=gain.at[source], dst_ref=gain.at[source],
            send_sem=nsend.at[n], recv_sem=nrecv.at[n], device_id=other(i, j), device_id_type=MESH,
        )

    def step(c, _):
        @pl.when(c + 1 < chunks)
        def _():
            stage_a(c + 1)

        stage_b(c)

        @pl.when(c >= LAG)
        def _():
            stage_c(c - LAG)

        return 0

    lax.fori_loop(0, chunks, step, 0)
    for n, (i, j) in enumerate(everyone):
        gain_copy(n, i, j).start()
    lax.fori_loop(chunks - LAG, chunks, lambda c, _: (stage_c(c), 0)[1], 0)

    def finish(c, _):
        for k in range(3):
            share(c, k).wait_send()
        for k in range(2):
            give(c, k).wait_send()
            pass_on(c, k).wait_send()
            pass_in(c, k).wait_recv()
        keep(c).wait()
        save(c).wait()
        return 0

    lax.fori_loop(0, chunks, finish, 0)
    for n, (i, j) in enumerate(everyone):
        gain_copy(n, i, j).wait_send()
        gain_in(n, i, j).wait_recv()
    N[...] = gain[...]


def spread_kernel(chunks, T, R, fg, fu, rg, ru):
    for c in range(chunks):
        at = slice(c * LANES, (c + 1) * LANES)
        fg[:, at] = T[c, 0, 0]
        fu[:, at] = T[c, 0, 1]
        rg[:, at] = R[c, 0]
        ru[:, at] = R[c, 1]


def ringed(tg, dg, sg, tu, du, su, norm_train, norm_step, ncols):
    rows, width = tg.shape
    chunks = width // LANES
    small = norm_train.shape[0]
    peers = 4 * ncols - 1
    bf16, f32 = jnp.bfloat16, jnp.float32
    dma = pltpu.SemaphoreType.DMA
    any_spec = pl.BlockSpec(memory_space=pl.ANY)
    vmem = pl.BlockSpec(memory_space=pltpu.VMEM)
    T, R, col, N = pl.pallas_call(
        functools.partial(gather_kernel, chunks, ncols),
        out_shape=(
            jax.ShapeDtypeStruct((chunks, 4, 2, rows, LANES), bf16),
            jax.ShapeDtypeStruct((chunks, 2, rows, LANES), f32),
            jax.ShapeDtypeStruct((chunks, 2, LANES), f32),
            jax.ShapeDtypeStruct((4 * ncols, 1, small), bf16),
        ),
        in_specs=[any_spec] * 6 + [vmem] * 2,
        out_specs=(any_spec, any_spec, vmem, vmem),
        scratch_shapes=[
            pltpu.VMEM((2, 6, rows, LANES), f32),
            pltpu.VMEM((chunks, 2, rows, LANES), f32),
            pltpu.VMEM((chunks, 2, rows, LANES), bf16),
            pltpu.VMEM((chunks, 4, 2, LANES), f32),
            pltpu.VMEM((4 * ncols, 1, small), bf16),
            dma((2, 6)), dma((chunks,)), dma((chunks,)),
            dma((chunks, 3)), dma((chunks, 3)),
            dma((chunks, 2)), dma((chunks, 2)),
            dma((chunks, 2)), dma((chunks, 2)),
            dma((peers,)), dma((peers,)),
        ],
        compiler_params=pltpu.CompilerParams(
            collective_id=0, has_side_effects=True, vmem_limit_bytes=48 * 2**20
        ),
    )(tg, dg, sg, tu, du, su, norm_train.reshape(1, small), norm_step.reshape(1, small))

    steps = 5
    block = rows // steps
    thin = rows // (4 * steps)
    fg, fu, rg, ru = pl.pallas_call(
        functools.partial(spread_kernel, chunks),
        grid=(4, steps),
        out_shape=(
            jax.ShapeDtypeStruct((4 * rows, width), bf16),
            jax.ShapeDtypeStruct((4 * rows, width), bf16),
            jax.ShapeDtypeStruct((rows, width), f32),
            jax.ShapeDtypeStruct((rows, width), f32),
        ),
        in_specs=[
            pl.BlockSpec((chunks, 1, 2, block, LANES), lambda s, r: (0, s, 0, r, 0)),
            pl.BlockSpec((chunks, 2, thin, LANES), lambda s, r: (0, 0, s * steps + r, 0)),
        ],
        out_specs=(
            pl.BlockSpec((block, width), lambda s, r: (s * steps + r, 0)),
            pl.BlockSpec((block, width), lambda s, r: (s * steps + r, 0)),
            pl.BlockSpec((thin, width), lambda s, r: (s * steps + r, 0)),
            pl.BlockSpec((thin, width), lambda s, r: (s * steps + r, 0)),
        ),
    )(T, R)
    return (
        fg, fu, col[:, 0].reshape(width), col[:, 1].reshape(width), N.reshape(4 * ncols * small), rg, ru
    )


def solution(mesh):
    ncols = mesh.shape["cols"]

    def local(*args):
        rows, width = args[0].shape
        if mesh.shape["shard"] == 4 and width % LANES == 0 and rows % 320 == 0 and width // LANES > LAG:
            return ringed(*args, ncols)
        return plain(*args)

    return jax.shard_map(
        local,
        mesh=mesh,
        in_specs=(P(("copy", "shard"), "cols"),) * 6 + (P(("copy", "shard", "cols")),) * 2,
        out_specs=(
            P("copy", "cols"),
            P("copy", "cols"),
            P(("copy", "cols")),
            P(("copy", "cols")),
            P("copy"),
            P(("copy", "shard"), "cols"),
            P(("copy", "shard"), "cols"),
        ),
        check_vma=False,
    )
```

time: 320 us -> 251 us (0.78)
  Pallas kernels: 0 us -> 247 us
  waiting for transfers between devices: 197 us -> 0 us
  blocking collectives: 60 us -> 0 us
  other arithmetic: 29.6 us -> 0.05 us
  local copies, waits for them, and re-layouts: 18.4 us -> 2.68 us
  between operations: 14.8 us -> 0.65 us
    pallas_call x0 -> x2, Pallas kernels: none -> 247 us  [the longest x1 215 us: ringed(): pl.pallas_call(functools.partial(gather_kernel, chunks, ncols), out_shape...]
    all_gather x2 -> x0, waiting for transfers between devices: 197 us -> none  [the longest x1 124 us: local(): lax.all_gather(narrow_gate, 'shard', axis=0, tiled=True)]
    unnamed x1 -> x0, blocking collectives: 42.3 us -> none
    reduce_sum x1 -> x0, other arithmetic: 19.9 us -> none  [local(): jnp.sum(result_up * result_up, axis=0)]
    psum x1 -> x0, blocking collectives: 17.7 us -> none  [local(): lax.psum((jnp.sum(result_gate * result_gate, axis=0), jnp.sum(result_up *...]
    unnamed x17 -> x4, local copies, waits for them, and re-layouts: 18.4 us -> 1.35 us
    convert_element_type x3 -> x0, other arithmetic: 9.69 us -> none  [the longest x1 4.85 us: local(): (result_gate / column_gate).astype(jnp.bfloat16)]
  transfers between devices with their start and end apart: 2 -> 0, of which waited for: 2 -> 0; matrix products, arithmetic and copies ran while one was open for 2% -> 0% of each run, Pallas kernels for 0% -> 0%
where the time goes in v1:
time: 251 us
  Pallas kernels  247 us (98%)
  local copies, waits for them, and re-layouts  2.68 us (1%)
    pallas_call x1, Pallas kernels, ringed(): pl.pallas_call(functools.partial(gather_kernel, chunks, ncols), out_shape...  215 us
    pallas_call x1, Pallas kernels, ringed(): pl.pallas_call(functools.partial(spread_kernel, chunks), grid=(4, steps),...  31.9 us

profile of v1, /device:TPU:0, one launch (start us, length us, event | category | flops | bytes accessed | tf_op | source)
XLA Modules:
  0.0 250.6 jit_solution(12750235974133096743)
XLA Ops:
  0.6 0.0 copy-start
  0.6 0.7 copy-done
  1.3 0.0 copy-start.1
  1.3 0.7 copy-done.1
  2.0 215.3 %shard_map.135 = (bf16[19,4,2,640,128]{4,3,2,1,0:T(8,128)(2,1)}, f32[19,2,640,128]{3,2,1,0:T(8,128)}, f32[19,2,128]{2,1,0:T(2,128)S(1)}, bf16[16,1,160]{2,1,0:T(2,128)(2,1)S(1)}) custom-call(f32[640,2432]{1,0:T(8,128)} %tg.1, f32[640,2432]{1,0:T(8,128)} %dg.1, f32[640,2432]{1,0:T(8,128)} %sg.1, f32[640,2432]{1,0:T(8,128)} %tu.1, f32[640,2432]{1,0:T(8,128)} %du.1, ...), custom_call_target="tpu_custom_call" | custom-call | tf_op jit(solution)/shard_map/pallas_call | solution.py:244
  217.3 31.9 %shard_map.136 = (bf16[2560,2432]{1,0:T(8,128)(2,1)}, bf16[2560,2432]{1,0:T(8,128)(2,1)}, f32[640,2432]{1,0:T(8,128)}, f32[640,2432]{1,0:T(8,128)}) custom-call(bf16[19,4,2,640,128]{4,3,2,1,0:T(8,128)(2,1)} %get-tuple-element.15.T, f32[19,2,640,128]{3,2,1,0:T(8,128)} %get-tuple-element.16.R), custom_call_target="tpu_custom_call" | custom-call | tf_op jit(solution)/shard_map/pallas_call | solution.py:274
  249.2 0.1 reduce.2
  249.2 0.7 reshape.25
  249.9 0.6 slice_reduce_fusion
Async XLA Ops:
  0.6 0.7 copy-start
  1.3 0.7 copy-start.1

commit v2 on v1

--- a/solution.py
+++ b/solution.py
@@ -13,6 +13,7 @@
 LANES = 128
 BLOCK = 64
 LAG = 3
+TAIL = 3
 MESH = pl.DeviceIdType.MESH
 
 
@@ -46,11 +47,12 @@
 def gather_kernel(
     chunks, ncols,
     tg, dg, sg, tu, du, su, norm_a, norm_b,
-    T, R, col, N,
+    T, R, Og, Ou, col, N,
     inbuf, res, own, part, gain,
-    in_sem, res_sem, loc_sem, psend, precv, osend, orecv, fsend, frecv, nsend, nrecv,
+    in_sem, res_sem, loc_sem, tail_sem, psend, precv, osend, orecv, fsend, frecv, nsend, nrecv,
 ):
     ins = (tg, dg, sg, tu, du, su)
+    lead = T.shape[0]
     rows = tg.shape[0]
     me = lax.axis_index("shard")
     mc = lax.axis_index("cols")
@@ -120,6 +122,12 @@
     def keep(c):
         return pltpu.make_async_copy(own.at[c], T.at[c, me], loc_sem.at[c])
 
+    def leave(c):
+        return [
+            pltpu.make_async_copy(own.at[lead + c, g], out.at[c], tail_sem.at[c, g])
+            for g, out in enumerate((Og, Ou))
+        ]
+
     def stage_a(c):
         slot = lax.rem(c, 2)
         for f in fetch(c, slot):
@@ -159,9 +167,17 @@
                 return 0
 
             lax.fori_loop(0, rows // BLOCK, body, 0)
-        for k in range(2):
-            give(c, k).start()
-        keep(c).start()
+
+        @pl.when(c < lead)
+        def _():
+            for k in range(2):
+                give(c, k).start()
+            keep(c).start()
+
+        @pl.when(c >= lead)
+        def _():
+            for copy in leave(c - lead):
+                copy.start()
 
     def stage_c(c):
         for k in range(2):
@@ -194,7 +210,7 @@
 
         stage_b(c)
 
-        @pl.when(c >= LAG)
+        @pl.when((c >= LAG) & (c < lead + LAG))
         def _():
             stage_c(c - LAG)
 
@@ -203,33 +219,59 @@
     lax.fori_loop(0, chunks, step, 0)
     for n, (i, j) in enumerate(everyone):
         gain_copy(n, i, j).start()
-    lax.fori_loop(chunks - LAG, chunks, lambda c, _: (stage_c(c), 0)[1], 0)
-
-    def finish(c, _):
+    if lead > chunks - LAG:
+        lax.fori_loop(chunks - LAG, lead, lambda c, _: (stage_c(c), 0)[1], 0)
+
+    def settle(c, _):
         for k in range(3):
             share(c, k).wait_send()
+        save(c).wait()
+        return 0
+
+    def finish(c, _):
         for k in range(2):
             give(c, k).wait_send()
             pass_on(c, k).wait_send()
             pass_in(c, k).wait_recv()
         keep(c).wait()
-        save(c).wait()
         return 0
 
-    lax.fori_loop(0, chunks, finish, 0)
+    lax.fori_loop(0, chunks, settle, 0)
+    for c in range(chunks - lead):
+        for copy in leave(c):
+            copy.wait()
+    lax.fori_loop(0, lead, finish, 0)
     for n, (i, j) in enumerate(everyone):
         gain_copy(n, i, j).wait_send()
         gain_in(n, i, j).wait_recv()
     N[...] = gain[...]
 
 
-def spread_kernel(chunks, T, R, fg, fu, rg, ru):
-    for c in range(chunks):
+def lead_kernel(lead, T, fg, fu):
+    for c in range(lead):
         at = slice(c * LANES, (c + 1) * LANES)
         fg[:, at] = T[c, 0, 0]
         fu[:, at] = T[c, 0, 1]
+
+
+def result_kernel(chunks, R, rg, ru):
+    for c in range(chunks):
+        at = slice(c * LANES, (c + 1) * LANES)
         rg[:, at] = R[c, 0]
         ru[:, at] = R[c, 1]
+
+
+def near_kernel(place, og, ou, xg, xu, yg, yu, held_g, held_u, fg, fu):
+    for j, (gate, up) in enumerate(((og, ou), (xg, xu), (yg, yu))):
+        @pl.when(pl.program_id(1) == j)
+        def _():
+            fg[...] = gate[0]
+            fu[...] = up[0]
+
+
+def far_kernel(place, g, u, held_g, held_u, fg, fu):
+    fg[...] = g[0]
+    fu[...] = u[0]
 
 
 def ringed(tg, dg, sg, tu, du, su, norm_train, norm_step, ncols):
@@ -241,26 +283,29 @@
     dma = pltpu.SemaphoreType.DMA
     any_spec = pl.BlockSpec(memory_space=pl.ANY)
     vmem = pl.BlockSpec(memory_space=pltpu.VMEM)
-    T, R, col, N = pl.pallas_call(
+    lead = chunks - TAIL
+    T, R, Og, Ou, col, N = pl.pallas_call(
         functools.partial(gather_kernel, chunks, ncols),
         out_shape=(
-            jax.ShapeDtypeStruct((chunks, 4, 2, rows, LANES), bf16),
+            jax.ShapeDtypeStruct((lead, 4, 2, rows, LANES), bf16),
             jax.ShapeDtypeStruct((chunks, 2, rows, LANES), f32),
+            jax.ShapeDtypeStruct((TAIL, rows, LANES), bf16),
+            jax.ShapeDtypeStruct((TAIL, rows, LANES), bf16),
             jax.ShapeDtypeStruct((chunks, 2, LANES), f32),
             jax.ShapeDtypeStruct((4 * ncols, 1, small), bf16),
         ),
         in_specs=[any_spec] * 6 + [vmem] * 2,
-        out_specs=(any_spec, any_spec, vmem, vmem),
+        out_specs=(any_spec,) * 4 + (vmem,) * 2,
         scratch_shapes=[
             pltpu.VMEM((2, 6, rows, LANES), f32),
             pltpu.VMEM((chunks, 2, rows, LANES), f32),
             pltpu.VMEM((chunks, 2, rows, LANES), bf16),
             pltpu.VMEM((chunks, 4, 2, LANES), f32),
             pltpu.VMEM((4 * ncols, 1, small), bf16),
-            dma((2, 6)), dma((chunks,)), dma((chunks,)),
+            dma((2, 6)), dma((chunks,)), dma((lead,)), dma((TAIL, 2)),
             dma((chunks, 3)), dma((chunks, 3)),
-            dma((chunks, 2)), dma((chunks, 2)),
-            dma((chunks, 2)), dma((chunks, 2)),
+            dma((lead, 2)), dma((lead, 2)),
+            dma((lead, 2)), dma((lead, 2)),
             dma((peers,)), dma((peers,)),
         ],
         compiler_params=pltpu.CompilerParams(
@@ -268,29 +313,67 @@
         ),
     )(tg, dg, sg, tu, du, su, norm_train.reshape(1, small), norm_step.reshape(1, small))
 
+    over_x = [(s, s ^ 1) for s in range(4)]
+    over_y = [(s, s ^ 2) for s in range(4)]
+    xg = lax.ppermute(Og, "shard", over_x)
+    yu = lax.ppermute(Ou, "shard", over_y)
+    xu = lax.ppermute(Ou, "shard", over_x)
+    yg = lax.ppermute(Og, "shard", over_y)
+
+    finals = (jax.ShapeDtypeStruct((4 * rows, width), bf16),) * 2
+    results = (jax.ShapeDtypeStruct((rows, width), f32),) * 2
     steps = 5
     block = rows // steps
-    thin = rows // (4 * steps)
-    fg, fu, rg, ru = pl.pallas_call(
-        functools.partial(spread_kernel, chunks),
+    cost = functools.partial(pl.CostEstimate, flops=0, transcendentals=0)
+    fg, fu = pl.pallas_call(
+        functools.partial(lead_kernel, lead),
         grid=(4, steps),
-        out_shape=(
-            jax.ShapeDtypeStruct((4 * rows, width), bf16),
-            jax.ShapeDtypeStruct((4 * rows, width), bf16),
-            jax.ShapeDtypeStruct((rows, width), f32),
-            jax.ShapeDtypeStruct((rows, width), f32),
+        out_shape=finals,
+        in_specs=[pl.BlockSpec((lead, 1, 2, block, LANES), lambda s, r: (0, s, 0, r, 0))],
+        out_specs=(pl.BlockSpec((block, lead * LANES), lambda s, r: (s * steps + r, 0)),) * 2,
+        cost_estimate=cost(bytes_accessed=32 * lead * rows * LANES),
+    )(T)
+    xg, yu, fg, fu = lax.optimization_barrier((xg, yu, fg, fu))
+    far_g = lax.ppermute(xg, "shard", over_y)
+    far_u = lax.ppermute(yu, "shard", over_x)
+    thin = rows // 10
+    rg, ru = pl.pallas_call(
+        functools.partial(result_kernel, chunks),
+        grid=(10,),
+        out_shape=results,
+        in_specs=[pl.BlockSpec((chunks, 2, thin, LANES), lambda r: (0, 0, r, 0))],
+        out_specs=(pl.BlockSpec((thin, width), lambda r: (r, 0)),) * 2,
+        cost_estimate=cost(bytes_accessed=16 * rows * width),
+    )(R)
+
+    me = lax.axis_index("shard")
+    place = jnp.stack([me, me ^ 1, me ^ 2, me ^ 3]).astype(jnp.int32)
+    piece = pl.BlockSpec((1, rows, LANES), lambda c, j, p: (c, 0, 0))
+    fg, fu = pl.pallas_call(
+        near_kernel,
+        grid_spec=pltpu.PrefetchScalarGridSpec(
+            num_scalar_prefetch=1,
+            grid=(TAIL, 3),
+            in_specs=[piece] * 6 + [any_spec] * 2,
+            out_specs=(pl.BlockSpec((rows, LANES), lambda c, j, p: (p[j], lead + c)),) * 2,
         ),
-        in_specs=[
-            pl.BlockSpec((chunks, 1, 2, block, LANES), lambda s, r: (0, s, 0, r, 0)),
-            pl.BlockSpec((chunks, 2, thin, LANES), lambda s, r: (0, 0, s * steps + r, 0)),
-        ],
-        out_specs=(
-            pl.BlockSpec((block, width), lambda s, r: (s * steps + r, 0)),
-            pl.BlockSpec((block, width), lambda s, r: (s * steps + r, 0)),
-            pl.BlockSpec((thin, width), lambda s, r: (s * steps + r, 0)),
-            pl.BlockSpec((thin, width), lambda s, r: (s * steps + r, 0)),
+        out_shape=finals,
+        input_output_aliases={7: 0, 8: 1},
+        cost_estimate=cost(bytes_accessed=24 * TAIL * rows * LANES),
+    )(place, Og, Ou, xg, xu, yg, yu, fg, fu)
+    piece = pl.BlockSpec((1, rows, LANES), lambda c, p: (c, 0, 0))
+    fg, fu = pl.pallas_call(
+        far_kernel,
+        grid_spec=pltpu.PrefetchScalarGridSpec(
+            num_scalar_prefetch=1,
+            grid=(TAIL,),
+            in_specs=[piece] * 2 + [any_spec] * 2,
+            out_specs=(pl.BlockSpec((rows, LANES), lambda c, p: (p[3], lead + c)),) * 2,
         ),
-    )(T, R)
+        out_shape=finals,
+        input_output_aliases={3: 0, 4: 1},
+        cost_estimate=cost(bytes_accessed=8 * TAIL * rows * LANES),
+    )(place, far_g, far_u, fg, fu)
     return (
         fg, fu, col[:, 0].reshape(width), col[:, 1].reshape(width), N.reshape(4 * ncols * small), rg, ru
     )
@@ -301,7 +384,7 @@
 
     def local(*args):
         rows, width = args[0].shape
-        if mesh.shape["shard"] == 4 and width % LANES == 0 and rows % 320 == 0 and width // LANES > LAG:
+        if mesh.shape["shard"] == 4 and width % LANES == 0 and rows % 320 == 0 and width // LANES > LAG + TAIL:
             return ringed(*args, ncols)
         return plain(*args)
 

time: 251 us -> 246 us (0.980)
  Pallas kernels: 247 us -> 232 us
  starting transfers between devices: 0 us -> 6.73 us
    pallas_call x1, Pallas kernels: 215 us -> 184 us  [ringed(): pl.pallas_call(functools.partial(gather_kernel, chunks, ncols), out_shape...]
    pallas_call x1 -> x4, Pallas kernels: 31.9 us -> 47.4 us  [the longest x1 23.6 us: ringed(): pl.pallas_call(functools.partial(lead_kernel, lead), grid=(4, steps), out...]
    ppermute x0 -> x6, starting transfers between devices: none -> 6.73 us  [the longest x1 1.35 us: ringed(): far_u = lax.ppermute(yu, 'shard', over_x)]
  transfers between devices with their start and end apart: 0 -> 6, of which waited for: 0 -> 0; matrix products, arithmetic and copies ran while one was open for 0% -> 1% of each run, Pallas kernels for 0% -> 18%
where the time goes in v2:
time: 246 us; the launch traced here: 245 us
  Pallas kernels  232 us (94%)
  starting transfers between devices  6.73 us (3%)
  local copies, waits for them, and re-layouts  4.99 us (2%)
    pallas_call x1, Pallas kernels, ringed(): pl.pallas_call(functools.partial(gather_kernel, chunks, ncols), out_shape...  184 us
    pallas_call x1, Pallas kernels, ringed(): pl.pallas_call(functools.partial(lead_kernel, lead), grid=(4, steps), out...  23.6 us
    pallas_call x1, Pallas kernels, ringed(): pl.pallas_call(functools.partial(result_kernel, chunks), grid=(10,), out_...  12.2 us
    pallas_call x1, Pallas kernels, ringed(): pl.pallas_call(near_kernel, grid_spec=pltpu.PrefetchScalarGridSpec(num_sc...  7.81 us
  transfers between devices with their start and end apart: 6, of which 0 were waited for; matrix products, arithmetic and copies ran while one was open for 1% of the time, Pallas kernels for 18%

profile of v2, /device:TPU:0, one launch (start us, length us, event | category | flops | bytes accessed | tf_op | source)
XLA Modules:
  0.0 244.7 jit_solution(6370931313902256092)
XLA Ops:
  0.6 0.7 copy-done.2
  1.3 0.7 copy-done.3
  2.0 184.2 %shard_map.135 = (bf16[16,4,2,640,128]{4,3,2,1,0:T(8,128)(2,1)}, f32[19,2,640,128]{3,2,1,0:T(8,128)}, bf16[3,640,128]{2,1,0:T(8,128)(2,1)S(1)}, bf16[3,640,128]{...) custom-call(f32[640,2432]{1,0:T(8,128)} %tg.1, f32[640,2432]{1,0:T(8,128)} %dg.1, ...), custom_call_target="tpu_custom_call" | custom-call | tf_op jit(solution)/shard_map/pallas_call | solution.py:287
  186.2 1.3 collective-permute-start
  187.5 1.3 collective-permute-start.1
  188.8 0.7 collective-permute-start.5
  189.5 0.8 collective-permute-start.4
  190.4 23.6 %shard_map.136 = (bf16[2560,2432]{1,0:T(8,128)(2,1)}, bf16[2560,2432]{1,0:T(8,128)(2,1)}) custom-call(bf16[16,4,2,640,128]{4,3,2,1,0:T(8,128)(2,1)} %get-tuple-element.27.T), custom_call_target="tpu_custom_call" | custom-call | bytes 41943040 | tf_op jit(solution)/shard_map/pallas_call | solution.py:328
  213.9 0.0 collective-permute-done.xg
  214.0 1.3 collective-permute-start.2
  215.2 1.4 collective-permute-start.3
  216.6 0.1 reduce.2
  216.6 0.7 reshape.25
  217.3 12.2 %shard_map.139 = (f32[640,2432]{1,0:T(8,128)}, f32[640,2432]{1,0:T(8,128)}) custom-call(f32[19,2,640,128]{3,2,1,0:T(8,128)} %get-tuple-element.40.R), custom_call_target="tpu_custom_call" | custom-call | bytes 24903680 | tf_op jit(solution)/shard_map/pallas_call | solution.py:340
  229.6 0.6 pad_add_fusion.place
  230.2 0.6 slice_reduce_fusion
  230.9 0.0 collective-permute-done.5.yg
  230.9 0.0 collective-permute-done.4.xu
  230.9 0.8 copy-done.6
  231.6 0.8 copy-done.7
  232.4 7.8 %shard_map.137 = (bf16[2560,2432]{1,0:T(8,128)(2,1)}, bf16[2560,2432]{1,0:T(8,128)(2,1)}) custom-call(s32[4]{0:T(128)} %pad_add_fusion.place, bf16[3,640,128]{2,1,0:T(8,128)(2,1)} %copy-done, bf16[3,640,128]{2,1,0:T(8,128)(2,1)} %copy-done.1, bf16[3,640,128]{2,1,0:T(8,128)(2,1)} %copy-done.4, ...), custom_call_target="tpu_custom_call", output_to_operand_aliasing={{0}: (7, {}), {1}: (8, {})} | custom-call | bytes 5898240 | tf_op jit(solution)/shard_map/pallas_call | solution.py:352
  240.2 0.0 collective-permute-done.2.g
  240.2 0.8 copy-done.8
  241.0 3.7 %shard_map.138 = (bf16[2560,2432]{1,0:T(8,128)(2,1)}, bf16[2560,2432]{1,0:T(8,128)(2,1)}) custom-call(s32[4]{0:T(128)} %pad_add_fusion.place, bf16[3,640,128]{2,1,0:T(8,128)(2,1)} %copy-done.8, bf16[3,640,128]{2,1,0:T(8,128)(2,1)} %collective-permute-done.3.u, ...), custom_call_target="tpu_custom_call", output_to_operand_aliasing={{0}: (3, {}), {1}: (4, {})} | custom-call | bytes 1966080 | tf_op jit(solution)/shard_map/pallas_call | solution.py:365
  (15 shorter events, 0.0 us)
Async XLA Ops:
  0.6 0.7 copy-start.2
  1.3 0.7 copy-start.3
  186.2 43.3 %copy-start = (bf16[3,640,128]{2,1,0:T(8,128)(2,1)}, bf16[3,640,128]{2,1,0:T(8,128)(2,1)S(1)}, u32[]{:S(2)}) copy-start(bf16[3,640,128]{2,1,0:T(8,128)(2,1)S(1)} %get-tuple-element.25.og) | copy-start | bytes 1474564
  186.2 43.3 %copy-start.1 = (bf16[3,640,128]{2,1,0:T(8,128)(2,1)}, bf16[3,640,128]{2,1,0:T(8,128)(2,1)S(1)}, u32[]{:S(2)}) copy-start(bf16[3,640,128]{2,1,0:T(8,128)(2,1)S(1)} %get-tuple-element.26.ou) | copy-start | bytes 1474564
  186.2 27.7 %collective-permute-start = (bf16[3,640,128]{2,1,0:T(8,128)(2,1)S(1)}, bf16[3,640,128]{2,1,0:T(8,128)(2,1)S(1)}, u32[]{:S(2)}, u32[]{:S(2)}) collective-permute-start(bf16[3,640,128]{2,1,0:T(8,128)(2,1)S(1)} %get-tuple-element.25.og), channel_id=1, source_target_pairs={{0,4},{4,0},{8,12},{12,8},{1,5},{5,1},{9,13},{13,9},{2,6},{6,2},{1... | collective-permute-start | bytes 1474568 | tf_op jit(solution)/shard_map/ppermute | solution.py:318
  187.5 26.4 %collective-permute-start.1 = (bf16[3,640,128]{2,1,0:T(8,128)(2,1)S(1)}, bf16[3,640,128]{2,1,0:T(8,128)(2,1)S(1)}, u32[]{:S(2)}, u32[]{:S(2)}) collective-permute-start(bf16[3,640,128]{2,1,0:T(8,128)(2,1)S(1)} %get-tuple-element.26.ou), channel_id=1, source_target_pairs={{0,8},{4,12},{8,0},{12,4},{1,9},{5,13},{9,1},{13,5},{2,10},{6,14},... | collective-permute-start | bytes 1474568 | tf_op jit(solution)/shard_map/ppermute | solution.py:319
  188.8 42.0 %collective-permute-start.5 = (bf16[3,640,128]{2,1,0:T(8,128)(2,1)S(1)}, bf16[3,640,128]{2,1,0:T(8,128)(2,1)S(1)}, u32[]{:S(2)}, u32[]{:S(2)}) collective-permute-start(bf16[3,640,128]{2,1,0:T(8,128)(2,1)S(1)} %get-tuple-element.25.og), channel_id=1, source_target_pairs={{0,8},{4,12},{8,0},{12,4},{1,9},{5,13},{9,1},{13,5},{2,10},{6,14},... | collective-permute-start | bytes 1474568 | tf_op jit(solution)/shard_map/ppermute | solution.py:321
  189.5 41.3 %collective-permute-start.4 = (bf16[3,640,128]{2,1,0:T(8,128)(2,1)S(1)}, bf16[3,640,128]{2,1,0:T(8,128)(2,1)S(1)}, u32[]{:S(2)}, u32[]{:S(2)}) collective-permute-start(bf16[3,640,128]{2,1,0:T(8,128)(2,1)S(1)} %get-tuple-element.26.ou), channel_id=1, source_target_pairs={{0,4},{4,0},{8,12},{12,8},{1,5},{5,1},{9,13},{13,9},{2,6},{6,2},{1... | collective-permute-start | bytes 1474568 | tf_op jit(solution)/shard_map/ppermute | solution.py:320
  213.9 16.9 %copy-start.4 = (bf16[3,640,128]{2,1,0:T(8,128)(2,1)}, bf16[3,640,128]{2,1,0:T(8,128)(2,1)S(1)}, u32[]{:S(2)}) copy-start(bf16[3,640,128]{2,1,0:T(8,128)(2,1)S(1)} %collective-permute-done.xg) | copy-start | bytes 1474564
  213.9 16.9 %copy-start.5 = (bf16[3,640,128]{2,1,0:T(8,128)(2,1)}, bf16[3,640,128]{2,1,0:T(8,128)(2,1)S(1)}, u32[]{:S(2)}) copy-start(bf16[3,640,128]{2,1,0:T(8,128)(2,1)S(1)} %collective-permute-done.1.yu) | copy-start | bytes 1474564
  214.0 26.3 %collective-permute-start.2 = (bf16[3,640,128]{2,1,0:T(8,128)(2,1)S(1)}, bf16[3,640,128]{2,1,0:T(8,128)(2,1)S(1)}, u32[]{:S(2)}, u32[]{:S(2)}) collective-permute-start(bf16[3,640,128]{2,1,0:T(8,128)(2,1)S(1)} %collective-permute-done.xg), channel_id=1, source_target_pairs={{0,8},{4,12},{8,0},{12,4},{1,9},{5,13},{9,1},{13,5},{2,10},{6,14},... | collective-permute-start | bytes 1474568 | tf_op jit(solution)/shard_map/ppermute | solution.py:337
  215.2 25.0 %collective-permute-start.3 = (bf16[3,640,128]{2,1,0:T(8,128)(2,1)S(1)}, bf16[3,640,128]{2,1,0:T(8,128)(2,1)}, u32[]{:S(2)}, u32[]{:S(2)}) collective-permute-start(bf16[3,640,128]{2,1,0:T(8,128)(2,1)S(1)} %collective-permute-done.1.yu), channel_id=1, source_target_pairs={{0,4},{4,0},{8,12},{12,8},{1,5},{5,1},{9,13},{13,9},{2,6},{6,2},{1... | collective-permute-start | bytes 1474568 | tf_op jit(solution)/shard_map/ppermute | solution.py:338
  230.9 0.8 copy-start.6
  231.6 0.8 copy-start.7
  240.2 0.8 copy-start.8

commit v3 on v2

--- a/solution.py
+++ b/solution.py
@@ -13,7 +13,7 @@
 LANES = 128
 BLOCK = 64
 LAG = 3
-TAIL = 3
+TAIL = 5
 MESH = pl.DeviceIdType.MESH
 
 
@@ -263,15 +263,19 @@
 
 def near_kernel(place, og, ou, xg, xu, yg, yu, held_g, held_u, fg, fu):
     for j, (gate, up) in enumerate(((og, ou), (xg, xu), (yg, yu))):
-        @pl.when(pl.program_id(1) == j)
-        def _():
-            fg[...] = gate[0]
-            fu[...] = up[0]
+        @pl.when(pl.program_id(0) == j)
+        def _():
+            for c in range(TAIL):
+                at = slice(c * LANES, (c + 1) * LANES)
+                fg[:, at] = gate[c]
+                fu[:, at] = up[c]
 
 
 def far_kernel(place, g, u, held_g, held_u, fg, fu):
-    fg[...] = g[0]
-    fu[...] = u[0]
+    for c in range(TAIL):
+        at = slice(c * LANES, (c + 1) * LANES)
+        fg[:, at] = g[c]
+        fu[:, at] = u[c]
 
 
 def ringed(tg, dg, sg, tu, du, su, norm_train, norm_step, ncols):
@@ -348,27 +352,39 @@
 
     me = lax.axis_index("shard")
     place = jnp.stack([me, me ^ 1, me ^ 2, me ^ 3]).astype(jnp.int32)
-    piece = pl.BlockSpec((1, rows, LANES), lambda c, j, p: (c, 0, 0))
+    half = rows // 2
+    wide = (pl.Element(half), pl.Element(TAIL * LANES))
+
+    def source(j):
+        return pl.BlockSpec(
+            (TAIL, half, LANES),
+            lambda i, r, p: (0, jnp.where(i == j, r, jnp.where(i < j, 0, 1)), 0),
+        )
+
     fg, fu = pl.pallas_call(
         near_kernel,
         grid_spec=pltpu.PrefetchScalarGridSpec(
             num_scalar_prefetch=1,
-            grid=(TAIL, 3),
-            in_specs=[piece] * 6 + [any_spec] * 2,
-            out_specs=(pl.BlockSpec((rows, LANES), lambda c, j, p: (p[j], lead + c)),) * 2,
+            grid=(3, 2),
+            in_specs=[source(j) for j in (0, 0, 1, 1, 2, 2)] + [any_spec] * 2,
+            out_specs=(
+                pl.BlockSpec(wide, lambda i, r, p: ((p[i] * 2 + r) * half, lead * LANES)),
+            ) * 2,
         ),
         out_shape=finals,
         input_output_aliases={7: 0, 8: 1},
         cost_estimate=cost(bytes_accessed=24 * TAIL * rows * LANES),
     )(place, Og, Ou, xg, xu, yg, yu, fg, fu)
-    piece = pl.BlockSpec((1, rows, LANES), lambda c, p: (c, 0, 0))
+    piece = pl.BlockSpec((TAIL, half, LANES), lambda r, p: (0, r, 0))
     fg, fu = pl.pallas_call(
         far_kernel,
         grid_spec=pltpu.PrefetchScalarGridSpec(
             num_scalar_prefetch=1,
-            grid=(TAIL,),
+            grid=(2,),
             in_specs=[piece] * 2 + [any_spec] * 2,
-            out_specs=(pl.BlockSpec((rows, LANES), lambda c, p: (p[3], lead + c)),) * 2,
+            out_specs=(
+                pl.BlockSpec(wide, lambda r, p: ((p[3] * 2 + r) * half, lead * LANES)),
+            ) * 2,
         ),
         out_shape=finals,
         input_output_aliases={3: 0, 4: 1},

time: 246 us -> 226 us (0.919)
  Pallas kernels: 232 us -> 211 us
  waiting for transfers between devices: 0.02 us -> 3.6 us
    pallas_call x1, Pallas kernels: 184 us -> 167 us  [ringed(): pl.pallas_call(functools.partial(gather_kernel, chunks, ncols), out_shape...]
    ppermute x1, waiting for transfers between devices: 0.01 us -> 3.58 us  [ringed(): far_g = lax.ppermute(xg, 'shard', over_y)]
    pallas_call x1, Pallas kernels: 23.6 us -> 21 us  [ringed(): pl.pallas_call(functools.partial(lead_kernel, lead), grid=(4, steps), out...]
  transfers between devices with their start and end apart: 6 -> 6, of which waited for: 0 -> 1; matrix products, arithmetic and copies ran while one was open for 1% -> 1% of each run, Pallas kernels for 18% -> 18%
where the time goes in v3:
time: 226 us; the launch traced here: 225 us
  Pallas kernels  211 us (93%)
  starting transfers between devices  6.25 us (3%)
  waiting for transfers between devices  3.6 us (2%)
  local copies, waits for them, and re-layouts  2.7 us (1%)
    pallas_call x1, Pallas kernels, ringed(): pl.pallas_call(functools.partial(gather_kernel, chunks, ncols), out_shape...  167 us
    pallas_call x1, Pallas kernels, ringed(): pl.pallas_call(functools.partial(lead_kernel, lead), grid=(4, steps), out...  21 us
    pallas_call x1, Pallas kernels, ringed(): pl.pallas_call(functools.partial(result_kernel, chunks), grid=(10,), out_...  12.2 us
    pallas_call x1, Pallas kernels, ringed(): pl.pallas_call(near_kernel, grid_spec=pltpu.PrefetchScalarGridSpec(num_sc...  7.64 us
  transfers between devices with their start and end apart: 6, of which 1 were waited for; matrix products, arithmetic and copies ran while one was open for 1% of the time, Pallas kernels for 18%

profile of v3, /device:TPU:0, one launch (start us, length us, event | category | flops | bytes accessed | tf_op | source)
XLA Modules:
  0.0 225.1 jit_solution(5472991069805300972)
XLA Ops:
  0.6 0.0 copy-start.2
  0.6 0.7 copy-done.2
  1.3 0.7 copy-done.3
  2.0 167.2 %shard_map.135 = (bf16[14,4,2,640,128]{4,3,2,1,0:T(8,128)(2,1)}, f32[19,2,640,128]{3,2,1,0:T(8,128)}, bf16[5,640,128]{2,1,0:T(8,128)(2,1)S(1)}, bf16[5,640,128]{...) custom-call(f32[640,2432]{1,0:T(8,128)} %tg.1, f32[640,2432]{1,0:T(8,128)} %dg.1, ...), custom_call_target="tpu_custom_call" | custom-call | tf_op jit(solution)/shard_map/pallas_call | solution.py:291
  169.2 0.8 collective-permute-start
  170.0 1.3 collective-permute-start.1
  171.3 0.7 collective-permute-start.5
  172.0 1.3 collective-permute-start.4
  173.3 21.0 %shard_map.136 = (bf16[2560,2432]{1,0:T(8,128)(2,1)}, bf16[2560,2432]{1,0:T(8,128)(2,1)}) custom-call(bf16[14,4,2,640,128]{4,3,2,1,0:T(8,128)(2,1)} %get-tuple-element.27.T), custom_call_target="tpu_custom_call" | custom-call | bytes 36700160 | tf_op jit(solution)/shard_map/pallas_call | solution.py:332
  194.3 0.0 collective-permute-done.xg
  194.3 0.0 collective-permute-done.1.yu
  194.3 0.8 collective-permute-start.2
  195.1 1.4 collective-permute-start.3
  196.4 0.1 reduce.2
  196.5 0.7 reshape.25
  197.2 12.2 %shard_map.139 = (f32[640,2432]{1,0:T(8,128)}, f32[640,2432]{1,0:T(8,128)}) custom-call(f32[19,2,640,128]{3,2,1,0:T(8,128)} %get-tuple-element.40.R), custom_call_target="tpu_custom_call" | custom-call | bytes 24903680 | tf_op jit(solution)/shard_map/pallas_call | solution.py:344
  209.4 0.7 pad_add_fusion.place
  210.1 0.6 slice_reduce_fusion
  210.7 0.0 collective-permute-done.5.yg
  210.7 0.0 collective-permute-done.4.xu
  210.8 7.6 %shard_map.137 = (bf16[2560,2432]{1,0:T(8,128)(2,1)}, bf16[2560,2432]{1,0:T(8,128)(2,1)}) custom-call(s32[4]{0:T(128)} %pad_add_fusion.place, bf16[5,640,128]{2,1,0:T(8,128)(2,1)} %copy-done, bf16[5,640,128]{2,1,0:T(8,128)(2,1)} %copy-done.1, bf16[5,640,128]{2,1,0:T(8,128)(2,1)} %copy-done.4, ...), custom_call_target="tpu_custom_call", output_to_operand_aliasing={{0}: (7, {}), {1}: (8, {})} | custom-call | bytes 9830400 | tf_op jit(solution)/shard_map/pallas_call | solution.py:364
  218.4 3.6 %collective-permute-done.2.g = bf16[5,640,128]{2,1,0:T(8,128)(2,1)} collective-permute-done((bf16[5,640,128]{2,1,0:T(8,128)(2,1)S(1)}, bf16[5,640,128]{2,1,0:T(8,128)(2,1)}, u32[]{:S(2)}, u32[]{:S(2)}) %collective-permute-start.2) | collective-permute-done | bytes 819232 | tf_op jit(solution)/shard_map/ppermute | solution.py:341
  222.0 0.0 collective-permute-done.3.u
  222.0 3.1 %shard_map.138 = (bf16[2560,2432]{1,0:T(8,128)(2,1)}, bf16[2560,2432]{1,0:T(8,128)(2,1)}) custom-call(s32[4]{0:T(128)} %pad_add_fusion.place, bf16[5,640,128]{2,1,0:T(8,128)(2,1)} %collective-permute-done.2.g, bf16[5,640,128]{2,1,0:T(8,128)(2,1)} %collective-permute-done.3.u, ...), custom_call_target="tpu_custom_call", output_to_operand_aliasing={{0}: (3, {}), {1}: (4, {})} | custom-call | bytes 3276800 | tf_op jit(solution)/shard_map/pallas_call | solution.py:379
  (9 shorter events, 0.0 us)
Async XLA Ops:
  0.6 0.7 copy-start.2
  1.3 0.7 copy-start.3
  169.2 40.3 %copy-start = (bf16[5,640,128]{2,1,0:T(8,128)(2,1)}, bf16[5,640,128]{2,1,0:T(8,128)(2,1)S(1)}, u32[]{:S(2)}) copy-start(bf16[5,640,128]{2,1,0:T(8,128)(2,1)S(1)} %get-tuple-element.25.og) | copy-start | bytes 2457604
  169.2 40.3 %copy-start.1 = (bf16[5,640,128]{2,1,0:T(8,128)(2,1)}, bf16[5,640,128]{2,1,0:T(8,128)(2,1)S(1)}, u32[]{:S(2)}) copy-start(bf16[5,640,128]{2,1,0:T(8,128)(2,1)S(1)} %get-tuple-element.26.ou) | copy-start | bytes 2457604
  169.2 25.1 %collective-permute-start = (bf16[5,640,128]{2,1,0:T(8,128)(2,1)S(1)}, bf16[5,640,128]{2,1,0:T(8,128)(2,1)S(1)}, u32[]{:S(2)}, u32[]{:S(2)}) collective-permute-start(bf16[5,640,128]{2,1,0:T(8,128)(2,1)S(1)} %get-tuple-element.25.og), channel_id=1, source_target_pairs={{0,4},{4,0},{8,12},{12,8},{1,5},{5,1},{9,13},{13,9},{2,6},{6,2},{1... | collective-permute-start | bytes 2457608 | tf_op jit(solution)/shard_map/ppermute | solution.py:322
  170.0 24.3 %collective-permute-start.1 = (bf16[5,640,128]{2,1,0:T(8,128)(2,1)S(1)}, bf16[5,640,128]{2,1,0:T(8,128)(2,1)S(1)}, u32[]{:S(2)}, u32[]{:S(2)}) collective-permute-start(bf16[5,640,128]{2,1,0:T(8,128)(2,1)S(1)} %get-tuple-element.26.ou), channel_id=1, source_target_pairs={{0,8},{4,12},{8,0},{12,4},{1,9},{5,13},{9,1},{13,5},{2,10},{6,14},... | collective-permute-start | bytes 2457608 | tf_op jit(solution)/shard_map/ppermute | solution.py:323
  171.3 39.4 %collective-permute-start.5 = (bf16[5,640,128]{2,1,0:T(8,128)(2,1)S(1)}, bf16[5,640,128]{2,1,0:T(8,128)(2,1)}, u32[]{:S(2)}, u32[]{:S(2)}) collective-permute-start(bf16[5,640,128]{2,1,0:T(8,128)(2,1)S(1)} %get-tuple-element.25.og), channel_id=1, source_target_pairs={{0,8},{4,12},{8,0},{12,4},{1,9},{5,13},{9,1},{13,5},{2,10},{6,14},... | collective-permute-start | bytes 2457608 | tf_op jit(solution)/shard_map/ppermute | solution.py:325
  172.0 38.7 %collective-permute-start.4 = (bf16[5,640,128]{2,1,0:T(8,128)(2,1)S(1)}, bf16[5,640,128]{2,1,0:T(8,128)(2,1)}, u32[]{:S(2)}, u32[]{:S(2)}) collective-permute-start(bf16[5,640,128]{2,1,0:T(8,128)(2,1)S(1)} %get-tuple-element.26.ou), channel_id=1, source_target_pairs={{0,4},{4,0},{8,12},{12,8},{1,5},{5,1},{9,13},{13,9},{2,6},{6,2},{1... | collective-permute-start | bytes 2457608 | tf_op jit(solution)/shard_map/ppermute | solution.py:324
  194.3 16.5 %copy-start.4 = (bf16[5,640,128]{2,1,0:T(8,128)(2,1)}, bf16[5,640,128]{2,1,0:T(8,128)(2,1)S(1)}, u32[]{:S(2)}) copy-start(bf16[5,640,128]{2,1,0:T(8,128)(2,1)S(1)} %collective-permute-done.xg) | copy-start | bytes 2457604
  194.3 16.5 %copy-start.5 = (bf16[5,640,128]{2,1,0:T(8,128)(2,1)}, bf16[5,640,128]{2,1,0:T(8,128)(2,1)S(1)}, u32[]{:S(2)}) copy-start(bf16[5,640,128]{2,1,0:T(8,128)(2,1)S(1)} %collective-permute-done.1.yu) | copy-start | bytes 2457604
  194.3 27.7 %collective-permute-start.2 = (bf16[5,640,128]{2,1,0:T(8,128)(2,1)S(1)}, bf16[5,640,128]{2,1,0:T(8,128)(2,1)}, u32[]{:S(2)}, u32[]{:S(2)}) collective-permute-start(bf16[5,640,128]{2,1,0:T(8,128)(2,1)S(1)} %collective-permute-done.xg), channel_id=1, source_target_pairs={{0,8},{4,12},{8,0},{12,4},{1,9},{5,13},{9,1},{13,5},{2,10},{6,14},... | collective-permute-start | bytes 2457608 | tf_op jit(solution)/shard_map/ppermute | solution.py:341
  195.1 26.9 %collective-permute-start.3 = (bf16[5,640,128]{2,1,0:T(8,128)(2,1)S(1)}, bf16[5,640,128]{2,1,0:T(8,128)(2,1)}, u32[]{:S(2)}, u32[]{:S(2)}) collective-permute-start(bf16[5,640,128]{2,1,0:T(8,128)(2,1)S(1)} %collective-permute-done.1.yu), channel_id=1, source_target_pairs={{0,4},{4,0},{8,12},{12,8},{1,5},{5,1},{9,13},{13,9},{2,6},{6,2},{1... | collective-permute-start | bytes 2457608 | tf_op jit(solution)/shard_map/ppermute | solution.py:342
